TPU v7x, 32 devices: a whole 2x2x4 slice. The times are simulated.
32 devices in a mesh: col: 4 (over z), row: 2 (over y), depth: 4 (over x, core).
Axes of the slice: x: 2, y: 2, z: 4, core: 2. Of those that a mesh axis runs over, the one named last changes fastest.
Arguments:
- a_mat: bfloat16 [4096, 8192], P(('depth', 'row', 'col'))
- b_mat: bfloat16 [8192, 4608], P(('depth', 'row', 'col'))
Outputs:
- output: bfloat16 [4096, 4608], P(('depth', 'row', 'col'))
All inputs are finite; a program needn't handle non-finite values.
Results may differ from a plain program's by a relative error of at most 0.001.
Values are sent between devices in bfloat16 or wider.
A program may use at most 1 GiB of HBM per device.

v0:
```python
import jax
import jax.numpy as jnp
from jax import lax
from jax.sharding import PartitionSpec as P


def solution(mesh):
    all_axes = ("depth", "row", "col")
    depth_size = mesh.shape["depth"]
    col_size = mesh.shape["col"]

    def device_block(a_rows, b_rows):
        a_part = lax.all_to_all(a_rows, "depth", 1, 0, tiled=True)
        a_block = lax.all_gather(a_part, "col", axis=0, tiled=True)
        b_part = lax.all_to_all(b_rows, "col", 1, 0, tiled=True)
        b_block = lax.all_gather(b_part, "row", axis=0, tiled=True)
        part_sum = jnp.dot(a_block, b_block, preferred_element_type=jnp.float32)
        rows_dev = a_rows.shape[0]
        n_cols = part_sum.shape[1]
        grouped = part_sum.reshape(col_size, depth_size * rows_dev, n_cols)
        summed = lax.psum_scatter(grouped, "depth", scatter_dimension=1, tiled=True)
        rounded = summed.astype(jnp.bfloat16).reshape(col_size * rows_dev, n_cols)
        return lax.all_to_all(rounded, "col", 0, 1, tiled=True)

    return jax.shard_map(device_block, mesh=mesh, in_specs=(P(all_axes, None), P(all_axes, None)), out_specs=P(all_axes, None), check_vma=False)
```

profile of v0, /device:TPU:0, one launch (start us, length us, event | category | flops | bytes accessed | tf_op | source)
XLA Modules:
  0.0 420.8 jit_solution(8189574339901584292)
XLA Ops:
  6.5 0.0 all-gather.5.cloned.1.call-start
  6.5 4.3 %copy.7 = bf16[256,4608]{0,1:T(8,128)(2,1)} copy(bf16[256,4608]{1,0:T(8,128)(2,1)} %param.3) | data formatting | bytes 4718592 | tf_op args[1]
  10.8 60.0 %all_to_all.54 = bf16[256,4,1152]{0,2,1:T(8,128)(2,1)S(1)} all-to-all(bf16[256,4,1152]{0,2,1:T(8,128)(2,1)} %bitcast.15), channel_id=1, replica_groups=mesh['col'=4,'row'=2,'depth'=4] {'col'}, dimensions={1} | all-to-all | bytes 4718592 | tf_op jit(solution)/shard_map/all_to_all | solution.py:15
  70.8 2.5 copy.8
  73.3 0.0 copy-start
  73.3 0.0 all-gather.5.cloned.1.call-update
  73.3 0.0 all-gather.3.cloned.1.call-start
  73.4 1.5 copy-done
  74.9 2.4 copy.5
  77.3 29.0 %all_to_all.55 = bf16[128,4,2048]{0,2,1:T(8,128)(2,1)S(1)} all-to-all(bf16[128,4,2048]{0,2,1:T(8,128)(2,1)} %bitcast.18), channel_id=1, replica_groups=mesh['col'=4,'row'=2,'depth'=4] {'depth'}, dimensions={1} | all-to-all | bytes 4194304 | tf_op jit(solution)/shard_map/all_to_all | solution.py:13
  106.4 2.7 copy.6
  109.1 0.0 all-gather.3.cloned.1.call-update
  109.1 0.0 reduce-scatter.2.cloned.1.call-start
  109.1 26.4 %all-gather.5.cloned.1.call-done = bf16[2048,1152]{1,0:T(8,128)(2,1)} async-done(((bf16[1024,1152]{1,0:T(8,128)(2,1)}), bf16[2048,1152]{1,0:T(8,128)(2,1)}) %all-gather.5.cloned.1.call-update) | async-done | bytes 4718608 | tf_op jit(solution)/shard_map/all_gather | solution.py:16
  135.6 151.1 %all-gather.3.cloned.1.call-done = bf16[2048,2048]{1,0:T(8,128)(2,1)} async-done(((bf16[512,2048]{1,0:T(8,128)(2,1)}), bf16[2048,2048]{1,0:T(8,128)(2,1)}) %all-gather.3.cloned.1.call-update) | async-done | bytes 8388624 | tf_op jit(solution)/shard_map/all_gather | solution.py:14
  286.7 16.3 %fusion = f32[2048,1152]{1,0:T(8,128)} fusion(bf16[2048,2048]{1,0:T(8,128)(2,1)} %all-gather.3.cloned.1.call-done, bf16[2048,1152]{1,0:T(8,128)(2,1)} %all-gather.5.cloned.1.call-done), kind=kOutput, calls=%fused_computation | convolution fusion | flops 9663676416 | bytes 22544384 | tf_op jit(solution)/shard_map/dot_general | solution.py:17
  303.0 0.0 reduce-scatter.2.cloned.1.call-update
  303.0 75.6 %reduce-scatter.2.cloned.1.call-done = f32[4,128,1152]{2,1,0:T(8,128)} async-done(((f32[4,512,1152]{2,1,0:T(8,128)}), f32[4,128,1152]{2,1,0:T(8,128)}) %reduce-scatter.2.cloned.1.call-update) | async-done | bytes 2359312 | tf_op jit(solution)/shard_map/reduce_scatter | solution.py:21
  378.6 1.8 convert_element_type.3
  380.4 32.7 %all_to_all.56 = bf16[4,128,1152]{2,1,0:T(8,128)(2,1)S(1)} all-to-all(bf16[4,128,1152]{2,1,0:T(8,128)(2,1)S(1)} %convert_element_type.3), channel_id=1, replica_groups=mesh['col'=4,'row'=2,'depth'=4] {'col'}, dimensions={0} | all-to-all | bytes 2359296 | tf_op jit(solution)/shard_map/all_to_all | solution.py:23
  413.2 1.1 copy.10
Async XLA Ops:
  6.5 129.0 %all-gather.5.cloned.1.call-start = ((), (), s32[]{:S(2)}) async-start(), calls=%async_computation.5 | async-start | bytes 7077888 | tf_op jit(solution)/shard_map/all_gather | solution.py:16
  73.3 1.6 copy-start
  73.3 213.3 %all-gather.3.cloned.1.call-start = ((), (), s32[]{:S(2)}) async-start(), calls=%async_computation.4 | async-start | bytes 10485760 | tf_op jit(solution)/shard_map/all_gather | solution.py:14
  109.1 269.5 %reduce-scatter.2.cloned.1.call-start = ((), (), s32[]{:S(2)}) async-start(), calls=%async_computation.6 | async-start | bytes 11796480 | tf_op jit(solution)/shard_map/reduce_scatter | solution.py:21
Sparse Core Ops, SparseCore 0:
  73.5 62.0 all-gather.4
  137.1 149.4 all-gather.2
  303.1 75.4 reduce-scatter.1
where the time goes:
time: 421 us
  waiting for transfers between devices  253 us (60%)
  blocking collectives  122 us (29%)
  matrix products  16.3 us (4%)
  local copies, waits for them, and re-layouts  14.5 us (3%)
  between operations  13.1 us (3%)
    all_gather x1, waiting for transfers between devices, device_block(): a_block = lax.all_gather(a_part, 'col', axis=0, tiled=True)  151 us
    reduce_scatter x1, waiting for transfers between devices, device_block(): summed = lax.psum_scatter(grouped, 'depth', scatter_dimension=1, tiled=True)  75.6 us
    all_to_all x1, blocking collectives, device_block(): b_part = lax.all_to_all(b_rows, 'col', 1, 0, tiled=True)  60 us
    all_to_all x1, blocking collectives, device_block(): return lax.all_to_all(rounded, 'col', 0, 1, tiled=True)  32.7 us
    all_to_all x1, blocking collectives, device_block(): a_part = lax.all_to_all(a_rows, 'depth', 1, 0, tiled=True)  29 us
    all_gather x1, waiting for transfers between devices, device_block(): b_block = lax.all_gather(b_part, 'row', axis=0, tiled=True)  26.4 us
    dot_general x1, matrix products, device_block(): part_sum = jnp.dot(a_block, b_block, preferred_element_type=jnp.float32)  16.3 us
  transfers between devices with their start and end apart: 3, of which 3 were waited for; matrix products, arithmetic and copies ran while one was open for 1% of the time, Pallas kernels for 0%

commit v1 on v0

v1 whole, which is shorter than its diff:
```python
import functools

import jax
import jax.numpy as jnp
from jax import lax
from jax.experimental import pallas as pl
from jax.experimental.pallas import tpu as pltpu
from jax.sharding import PartitionSpec as P

MESH = pl.DeviceIdType.MESH
NC = 256
AHEAD = 2


def kernel(n_cols, a_ref, b_ref, c_ref, abuf, bbuf, pbuf, rbuf, obuf, a_loc, b_loc, a_snd, a_rcv, up_snd, up_rcv, dn_snd, dn_rcv, x_snd, x_rcv, r_snd, r_rcv, o_sem):
    depth, y, z = lax.axis_index("depth"), lax.axis_index("row"), lax.axis_index("col")
    x, core = depth // 2, depth % 2
    n_chunks = n_cols // NC
    rows_a = a_ref.shape[0]
    rows_b = b_ref.shape[0]
    half = 4 * rows_b

    up = (z + 1, y, depth)
    down = (z - 1, y, depth)
    twin = (z, y, 2 * x + 1 - core)
    x_peer = (z, y, 2 * (1 - x) + core)
    y_peer = (z, 1 - y, depth)
    diag = (z, 1 - y, 2 * (1 - x) + core)
    plane = (x_peer, y_peer, diag)
    plane_xy = ((1 - x, y), (x, 1 - y), (1 - x, 1 - y))

    def cols(j):
        return pl.ds(pl.multiple_of(j * NC, NC), NC)

    own_rows = pl.ds(pl.multiple_of(core * half + z * rows_b, rows_b), rows_b)
    load_b = pltpu.make_async_copy(b_ref, bbuf.at[own_rows], b_loc)
    load_b.start()

    def a_cols(px, py, k):
        return pl.ds(pl.multiple_of(((2 * px + k) * 2 + py) * half, half), half)

    my_group = pl.ds(pl.multiple_of((2 * x + y) * rows_a, rows_a), rows_a)
    load_a = []
    for k in range(2):
        load_a.append(pltpu.make_async_copy(a_ref.at[:, a_cols(x, y, k)], abuf.at[my_group, pl.ds(k * half, half)], a_loc.at[k]))
        load_a[-1].start()

    barrier = pltpu.get_barrier_semaphore()
    for peer in plane + (twin,):
        pl.semaphore_signal(barrier, inc=1, device_id=peer, device_id_type=MESH)

    @pl.when(z < 3)
    def _():
        pl.semaphore_signal(barrier, inc=1, device_id=up, device_id_type=MESH)

    @pl.when(z > 0)
    def _():
        pl.semaphore_signal(barrier, inc=1, device_id=down, device_id_type=MESH)

    @pl.when((z > 0) & (z < 3))
    def _():
        pl.semaphore_wait(barrier, 6)

    @pl.when((z == 0) | (z == 3))
    def _():
        pl.semaphore_wait(barrier, 5)

    def a_copy(i, k):
        px, py = plane_xy[i]
        return pltpu.make_async_remote_copy(
            a_ref.at[:, a_cols(px, py, k)], abuf.at[my_group, pl.ds(k * half, half)],
            a_snd.at[2 * i + k], a_rcv.at[2 * i + k], device_id=plane[i], device_id_type=MESH)

    def z_copy(h, j, target, snd, rcv, src):
        rows = pl.ds(pl.multiple_of(core * half + src * rows_b, rows_b), rows_b)
        return pltpu.make_async_remote_copy(
            bbuf.at[rows, cols(j)], bbuf.at[rows, cols(j)],
            snd.at[h, j], rcv.at[h, j], device_id=target, device_id_type=MESH)

    def up_send(h, j):
        return z_copy(h, j, up, up_snd, up_rcv, z - h)

    def up_recv(h, j):
        return z_copy(h, j, up, up_snd, up_rcv, z - 1 - h)

    def dn_send(h, j):
        return z_copy(h, j, down, dn_snd, dn_rcv, z + h)

    def dn_recv(h, j):
        return z_copy(h, j, down, dn_snd, dn_rcv, z + 1 + h)

    def twin_copy(j, who):
        rows = pl.ds(pl.multiple_of(who * half, half), half)
        return pltpu.make_async_remote_copy(
            bbuf.at[rows, cols(j)], bbuf.at[rows, cols(j)],
            x_snd.at[j], x_rcv.at[j], device_id=twin, device_id_type=MESH)

    def r_copy(i, j):
        px, py = plane_xy[i]
        return pltpu.make_async_remote_copy(
            pbuf.at[pl.ds(pl.multiple_of((2 * px + py) * rows_a, rows_a), rows_a), cols(j)], rbuf.at[i, :, cols(j)],
            r_snd.at[i, j], r_rcv.at[i, j], device_id=plane[i], device_id_type=MESH)

    def o_copy(j):
        return pltpu.make_async_copy(obuf.at[:, cols(j)], c_ref.at[:, cols(j)], o_sem.at[j])

    def send_own(j):
        @pl.when(z < 3)
        def _():
            up_send(0, j).start()

        @pl.when(z > 0)
        def _():
            dn_send(0, j).start()

    def relay(h, j):
        @pl.when(z >= h)
        def _():
            up_recv(h - 1, j).wait_recv()

        if h < 3:
            @pl.when((z >= h) & (z < 3))
            def _():
                up_send(h, j).start()

        @pl.when(z <= 3 - h)
        def _():
            dn_recv(h - 1, j).wait_recv()

        if h < 3:
            @pl.when((z <= 3 - h) & (z > 0))
            def _():
                dn_send(h, j).start()

    load_b.wait()
    for j in range(AHEAD):
        send_own(j)
    for i in range(3):
        for k in range(2):
            a_copy(i, k).start()

    def guarded(j, fn):
        @pl.when((j >= 0) & (j < n_chunks))
        def _():
            fn(j)

    def last_hop(j):
        relay(3, j)
        twin_copy(j, core).start()

    def multiply(j):
        @pl.when(j == 0)
        def _():
            for k in range(2):
                load_a[k].wait()
            for i in range(3):
                for k in range(2):
                    a_copy(i, k).wait_recv()

        twin_copy(j, 1 - core).wait_recv()
        pbuf[:, cols(j)] = jnp.dot(abuf[...], bbuf[:, cols(j)], preferred_element_type=jnp.float32)
        for i in (2, 0, 1):
            r_copy(i, j).start()

    def finish(j):
        for i in range(3):
            r_copy(i, j).wait_recv()
        total = pbuf[my_group, cols(j)] + rbuf[0, :, cols(j)] + rbuf[1, :, cols(j)] + rbuf[2, :, cols(j)]
        obuf[:, cols(j)] = total.astype(jnp.bfloat16)
        o_copy(j).start()

    @pl.loop(0, n_chunks + 5)
    def _(t):
        guarded(t + AHEAD, send_own)
        guarded(t, functools.partial(relay, 1))
        guarded(t - 1, functools.partial(relay, 2))
        guarded(t - 2, last_hop)
        guarded(t - 3, multiply)
        guarded(t - 5, finish)

    for i in range(3):
        for k in range(2):
            a_copy(i, k).wait_send()

    @pl.loop(0, n_chunks)
    def _(j):
        for h in range(3):
            @pl.when((z >= h) & (z < 3))
            def _():
                up_send(h, j).wait_send()

            @pl.when((z <= 3 - h) & (z > 0))
            def _():
                dn_send(h, j).wait_send()
        twin_copy(j, core).wait_send()
        for i in range(3):
            r_copy(i, j).wait_send()
        o_copy(j).wait()


def solution(mesh):
    all_axes = ("depth", "row", "col")

    def device_block(a_rows, b_rows):
        rows, depth = a_rows.shape
        rows_b, n_cols = b_rows.shape
        n = n_cols // NC
        dma = pltpu.SemaphoreType.DMA
        return pl.pallas_call(
            functools.partial(kernel, n_cols),
            out_shape=jax.ShapeDtypeStruct((rows, n_cols), jnp.bfloat16),
            in_specs=[pl.BlockSpec(memory_space=pl.ANY)] * 2,
            out_specs=pl.BlockSpec(memory_space=pl.ANY),
            scratch_shapes=[
                pltpu.VMEM((4 * rows, 8 * rows_b), jnp.bfloat16),
                pltpu.VMEM((8 * rows_b, n_cols), jnp.bfloat16),
                pltpu.VMEM((4 * rows, n_cols), jnp.float32),
                pltpu.VMEM((3, rows, n_cols), jnp.float32),
                pltpu.VMEM((rows, n_cols), jnp.bfloat16),
                dma((2,)), dma,
                dma((6,)), dma((6,)),
                dma((3, n)), dma((3, n)),
                dma((3, n)), dma((3, n)),
                dma((n,)), dma((n,)),
                dma((3, n)), dma((3, n)),
                dma((n,)),
            ],
            compiler_params=pltpu.CompilerParams(collective_id=0, has_side_effects=True, vmem_limit_bytes=62 * 2**20),
            name="product",
        )(a_rows, b_rows)

    return jax.shard_map(device_block, mesh=mesh, in_specs=(P(all_axes, None), P(all_axes, None)), out_specs=P(all_axes, None), check_vma=False)
```

time: 421 us -> 181 us (0.43)
  waiting for transfers between devices: 253 us -> 0 us
  Pallas kernels: 0 us -> 178 us
  blocking collectives: 122 us -> 0 us
  matrix products: 16.3 us -> 0 us
  between operations: 13.1 us -> 0.01 us
  local copies, waits for them, and re-layouts: 14.5 us -> 2.36 us
    pallas_call x0 -> x1, Pallas kernels: none -> 178 us  [device_block(): pl.pallas_call(functools.partial(kernel, n_cols), out_shape=jax.ShapeDtyp...]
    all_gather x2 -> x0, waiting for transfers between devices: 178 us -> none  [the longest x1 151 us: device_block(): a_block = lax.all_gather(a_part, 'col', axis=0, tiled=True)]
    all_to_all x3 -> x0, blocking collectives: 122 us -> none  [the longest x1 60 us: device_block(): b_part = lax.all_to_all(b_rows, 'col', 1, 0, tiled=True)]
    reduce_scatter x1 -> x0, waiting for transfers between devices: 75.6 us -> none  [device_block(): summed = lax.psum_scatter(grouped, 'depth', scatter_dimension=1, tiled=True)]
    dot_general x1 -> x0, matrix products: 16.3 us -> none  [device_block(): part_sum = jnp.dot(a_block, b_block, preferred_element_type=jnp.float32)]
    all_to_all x3 -> x0, local copies, waits for them, and re-layouts: 6.33 us -> none  [the longest x1 2.69 us: device_block(): a_part = lax.all_to_all(a_rows, 'depth', 1, 0, tiled=True)]
    unnamed x4 -> x1, local copies, waits for them, and re-layouts: 8.22 us -> 2.36 us
  transfers between devices with their start and end apart: 3 -> 0, of which waited for: 3 -> 0; matrix products, arithmetic and copies ran while one was open for 1% -> 0% of each run, Pallas kernels for 0% -> 0%
where the time goes in v1:
time: 181 us; the launch traced here: 180 us
  Pallas kernels  178 us (98%)
  local copies, waits for them, and re-layouts  2.36 us (1%)
    pallas_call x1, Pallas kernels, device_block(): pl.pallas_call(functools.partial(kernel, n_cols), out_shape=jax.ShapeDtyp...  178 us

profile of v1, /device:TPU:0, one launch (start us, length us, event | category | flops | bytes accessed | tf_op | source)
XLA Modules:
  0.0 180.5 jit_solution(18095685891660253844)
XLA Ops:
  0.0 178.1 %product.1 = bf16[128,4608]{1,0:T(8,128)(2,1)} custom-call(bf16[128,8192]{1,0:T(8,128)(2,1)} %a_ref.1, bf16[256,4608]{1,0:T(8,128)(2,1)} %b_ref.1), custom_call_target="tpu_custom_call" | custom-call | tf_op jit(solution)/shard_map/product/pallas_call | solution.py:209
  178.1 2.4 %copy.4 = bf16[128,4608]{1,0:T(8,128)(2,1)} copy(bf16[128,4608]{1,0:T(8,128)(2,1)} %product.1) | data formatting | bytes 2359296

commit v2 on v1

v2 whole, which is shorter than its diff:
```python
import functools

import jax
import jax.numpy as jnp
from jax import lax
from jax.experimental import pallas as pl
from jax.experimental.pallas import tpu as pltpu
from jax.sharding import PartitionSpec as P

MESH = pl.DeviceIdType.MESH
NC = 256
PERIOD = 4
JOBS = 4
FIRST_JOB = 12
AHEAD = 3
AHEAD_END = 6
LAG_MULTIPLY, LAG_MIDDLE, LAG_FINISH = 3, 4, 5


def kernel(
    n_cols, a_ref, b_ref, c_ref,
    abuf, abuf2, bbuf, pbuf, rx, ry, sx, sy, pbuf2, rx2, ry2, sx2, sy2, cbuf, obuf,
    a_loc, b_loc, a_snd, a_rcv, a2_snd, a2_rcv, up_snd, up_rcv, dn_snd, dn_rcv, t_snd, t_rcv,
    r_snd, r_rcv, q_snd, q_rcv, c_snd, c_rcv, o_sem,
):
    depth, y, z = lax.axis_index("depth"), lax.axis_index("row"), lax.axis_index("col")
    x, core = depth // 2, depth % 2
    n_chunks = n_cols // NC
    rows_a = a_ref.shape[0]
    rows_b = b_ref.shape[0]
    half = 4 * rows_b
    hr = rows_a // 2
    f32 = jnp.float32

    inner = (z == 1) | (z == 2)
    end = (z == 0) | (z == 3)
    up = (z + 1, y, depth)
    down = (z - 1, y, depth)
    partner = (z + 1 - 2 * (z % 2), y, depth)
    twin = (z, y, 2 * x + 1 - core)
    x_peer = (z, y, 2 * (1 - x) + core)
    y_peer = (z, 1 - y, depth)
    diag = (z, 1 - y, 2 * (1 - x) + core)
    plane = (x_peer, y_peer, diag)
    plane_xy = ((1 - x, y), (x, 1 - y), (1 - x, 1 - y))

    def cols(j):
        return pl.ds(pl.multiple_of(j * NC, NC), NC)

    def job_chunk(i):
        return PERIOD * i + PERIOD - 1

    def shared(j):
        return (j % PERIOD == PERIOD - 1) & (j < PERIOD * JOBS)

    def when(*conds):
        both = conds[0]
        for c in conds[1:]:
            both = both & c
        return pl.when(both)

    own_rows = pl.ds(pl.multiple_of(core * half + z * rows_b, rows_b), rows_b)
    load_b = pltpu.make_async_copy(b_ref, bbuf.at[own_rows], b_loc)
    load_b.start()

    def a_cols(px, py, k):
        return pl.ds(pl.multiple_of(((2 * px + k) * 2 + py) * half, half), half)

    my_group = pl.ds(pl.multiple_of((2 * x + y) * rows_a, rows_a), rows_a)
    load_a = []
    for k in range(2):
        load_a.append(pltpu.make_async_copy(a_ref.at[:, a_cols(x, y, k)], abuf.at[my_group, pl.ds(k * half, half)], a_loc.at[k]))
        load_a[-1].start()

    barrier = pltpu.get_barrier_semaphore()
    for peer in plane + (twin,):
        pl.semaphore_signal(barrier, inc=1, device_id=peer, device_id_type=MESH)

    @when(z < 3)
    def _():
        pl.semaphore_signal(barrier, inc=1, device_id=up, device_id_type=MESH)

    @when(z > 0)
    def _():
        pl.semaphore_signal(barrier, inc=1, device_id=down, device_id_type=MESH)

    @when(inner)
    def _():
        pl.semaphore_wait(barrier, 6)

    @when(end)
    def _():
        pl.semaphore_wait(barrier, 5)

    def remote(src, dst, snd, rcv, target):
        return pltpu.make_async_remote_copy(src, dst, snd, rcv, device_id=target, device_id_type=MESH)

    def a_copy(i, k):
        px, py = plane_xy[i]
        return remote(a_ref.at[:, a_cols(px, py, k)], abuf.at[my_group, pl.ds(k * half, half)], a_snd.at[2 * i + k], a_rcv.at[2 * i + k], plane[i])

    def a2_copy(i):
        rows = pl.ds(pl.multiple_of(i * rows_a, rows_a), rows_a)
        return remote(abuf.at[rows], abuf2.at[rows], a2_snd.at[i], a2_rcv.at[i], partner)

    def z_copy(h, j, target, snd, rcv, src):
        rows = pl.ds(pl.multiple_of(core * half + src * rows_b, rows_b), rows_b)
        return remote(bbuf.at[rows, cols(j)], bbuf.at[rows, cols(j)], snd.at[h, j], rcv.at[h, j], target)

    def up_send(h, j):
        return z_copy(h, j, up, up_snd, up_rcv, z - h)

    def up_recv(h, j):
        return z_copy(h, j, up, up_snd, up_rcv, z - 1 - h)

    def dn_send(h, j):
        return z_copy(h, j, down, dn_snd, dn_rcv, z + h)

    def dn_recv(h, j):
        return z_copy(h, j, down, dn_snd, dn_rcv, z + 1 + h)

    def sends_up(h, j):
        return (z >= h) & ((z < 2) | ((z == 2) & ~shared(j)))

    def sends_dn(h, j):
        return (z <= 3 - h) & ((z > 1) | ((z == 1) & ~shared(j)))

    def gets_up(h, j):
        return (z > h) & ((z < 3) | ~shared(j))

    def gets_dn(h, j):
        return (z < 3 - h) & ((z > 0) | ~shared(j))

    def works(j):
        return inner | ~shared(j)

    def twin_copy(j, who):
        rows = pl.ds(pl.multiple_of(who * half, half), half)
        return remote(bbuf.at[rows, cols(j)], bbuf.at[rows, cols(j)], t_snd.at[j], t_rcv.at[j], twin)

    low, high = pl.ds(0, hr), pl.ds(hr, hr)

    def stage1(own, s, j):
        p, bx, by = (pbuf, rx, ry) if own else (pbuf2, rx2, ry2)
        cs = cols(j)
        return (
            remote(p.at[1 - x, :, low, cs], bx.at[:, :, cs], r_snd.at[0, s], r_rcv.at[0, s], x_peer),
            remote(p.at[:, 1 - y, high, cs], by.at[:, :, cs], r_snd.at[1, s], r_rcv.at[1, s], y_peer),
        )

    def stage2(own, s, j):
        p, bx, by = (pbuf, sx, sy) if own else (pbuf2, sx2, sy2)
        cs = cols(j)
        return (
            remote(p.at[x, 1 - y, low, cs], by.at[:, cs], q_snd.at[0, s], q_rcv.at[0, s], y_peer),
            remote(p.at[1 - x, y, high, cs], bx.at[:, cs], q_snd.at[1, s], q_rcv.at[1, s], x_peer),
        )

    def partial(own, s, j, src):
        a, p = (abuf, pbuf) if own else (abuf2, pbuf2)
        cs = cols(j)
        p[:, :, :, cs] = jnp.dot(a[...], bbuf[:, cols(src)], preferred_element_type=f32).reshape(2, 2, rows_a, NC)
        for c in stage1(own, s, j):
            c.start()

    def middle(own, s, j):
        p, bx, by = (pbuf, rx, ry) if own else (pbuf2, rx2, ry2)
        cs = cols(j)
        one, two = stage1(own, s, j)
        fwd_y, fwd_x = stage2(own, s, j)
        one.wait_recv()
        p[x, 1 - y, low, cs] += bx[1 - y, :, cs]
        fwd_y.start()
        two.wait_recv()
        p[1 - x, y, high, cs] += by[1 - x, :, cs]
        fwd_x.start()

    def finish(own, s, j, dst):
        p, bx, by, qx, qy = (pbuf, rx, ry, sx, sy) if own else (pbuf2, rx2, ry2, sx2, sy2)
        out = obuf if own else cbuf
        cs = cols(j)
        for c in stage2(own, s, j):
            c.wait_recv()
        out[low, cs] = (p[x, y, low, cs] + bx[y, :, cs] + qy[:, cs]).astype(out.dtype)
        out[high, cs] = (p[x, y, high, cs] + by[x, :, cs] + qx[:, cs]).astype(out.dtype)

    def o_copy(j):
        return pltpu.make_async_copy(obuf.at[:, cols(j)], c_ref.at[:, cols(j)], o_sem.at[j])

    def c_copy(i):
        return remote(cbuf.at[:, cols(i)], obuf.at[:, cols(job_chunk(i))], c_snd.at[i], c_rcv.at[i], partner)

    def send_own(j):
        @when(sends_up(0, j))
        def _():
            up_send(0, j).start()

        @when(sends_dn(0, j))
        def _():
            dn_send(0, j).start()

    def relay(h, j):
        @when(gets_up(h - 1, j))
        def _():
            up_recv(h - 1, j).wait_recv()

        if h < 3:
            @when(sends_up(h, j))
            def _():
                up_send(h, j).start()

        @when(gets_dn(h - 1, j))
        def _():
            dn_recv(h - 1, j).wait_recv()

        if h < 3:
            @when(sends_dn(h, j))
            def _():
                dn_send(h, j).start()

    load_b.wait()
    for i in range(3):
        for k in range(2):
            a_copy(i, k).start()
    for j in range(AHEAD_END):
        when(end if j >= AHEAD else (z >= 0))(functools.partial(send_own, j))

    def in_range(j, count, fn, *more):
        when((j >= 0) & (j < count), *more)(lambda: fn(j))

    def last_hop(j):
        relay(3, j)

        @when(works(j))
        def _():
            twin_copy(j, core).start()

    def multiply(j):
        @when(j == 0)
        def _():
            for k in range(2):
                load_a[k].wait()
            for i in range(3):
                for k in range(2):
                    a_copy(i, k).wait_recv()

        @when(end, j < 4)
        def _():
            a2_copy(j).start()

        @when(works(j))
        def _():
            twin_copy(j, 1 - core).wait_recv()
            partial(True, j, j, j)

    def own_middle(j):
        when(works(j))(lambda: middle(True, j, j))

    def own_finish(j):
        @when(works(j))
        def _():
            finish(True, j, j, j)
            o_copy(j).start()

    def job_multiply(i):
        @when(i == 0)
        def _():
            for k in range(4):
                a2_copy(k).wait_recv()

        partial(False, n_chunks + i, i, job_chunk(i))

    def job_middle(i):
        middle(False, n_chunks + i, i)

    def job_finish(i):
        finish(False, n_chunks + i, i, i)
        c_copy(i).start()

    @pl.loop(0, n_chunks + LAG_FINISH)
    def _(t):
        in_range(t + AHEAD, n_chunks, send_own, inner)
        in_range(t + AHEAD_END, n_chunks, send_own, end)
        in_range(t, n_chunks, functools.partial(relay, 1))
        in_range(t - 1, n_chunks, functools.partial(relay, 2))
        in_range(t - 2, n_chunks, last_hop)
        in_range(t - LAG_MULTIPLY, n_chunks, multiply)
        in_range(t - LAG_MULTIPLY - FIRST_JOB, JOBS, job_multiply, inner)
        in_range(t - LAG_MIDDLE, n_chunks, own_middle)
        in_range(t - LAG_MIDDLE - FIRST_JOB, JOBS, job_middle, inner)
        in_range(t - LAG_FINISH, n_chunks, own_finish)
        in_range(t - LAG_FINISH - FIRST_JOB, JOBS, job_finish, inner)

    for i in range(3):
        for k in range(2):
            a_copy(i, k).wait_send()

    @when(end)
    def _():
        @pl.loop(0, JOBS)
        def _(i):
            c_copy(i).wait_recv()
            o_copy(job_chunk(i)).start()

        for i in range(4):
            a2_copy(i).wait_send()

    @when(inner)
    def _():
        @pl.loop(0, JOBS)
        def _(i):
            c_copy(i).wait_send()
            for c in stage1(False, n_chunks + i, i) + stage2(False, n_chunks + i, i):
                c.wait_send()

    @pl.loop(0, n_chunks)
    def _(j):
        for h in range(3):
            @when(sends_up(h, j))
            def _():
                up_send(h, j).wait_send()

            @when(sends_dn(h, j))
            def _():
                dn_send(h, j).wait_send()

        @when(works(j))
        def _():
            twin_copy(j, core).wait_send()
            for c in stage1(True, j, j) + stage2(True, j, j):
                c.wait_send()

        o_copy(j).wait()


def solution(mesh):
    all_axes = ("depth", "row", "col")

    def device_block(a_rows, b_rows):
        rows, depth = a_rows.shape
        rows_b, n_cols = b_rows.shape
        n = n_cols // NC
        hr = rows // 2
        nj = JOBS * NC
        dma = pltpu.SemaphoreType.DMA
        bf16, f32 = jnp.bfloat16, jnp.float32
        return pl.pallas_call(
            functools.partial(kernel, n_cols),
            out_shape=jax.ShapeDtypeStruct((rows, n_cols), bf16),
            in_specs=[pl.BlockSpec(memory_space=pl.ANY)] * 2,
            out_specs=pl.BlockSpec(memory_space=pl.ANY),
            scratch_shapes=[
                pltpu.VMEM((4 * rows, 8 * rows_b), bf16),
                pltpu.VMEM((4 * rows, 8 * rows_b), bf16),
                pltpu.VMEM((8 * rows_b, n_cols), bf16),
                pltpu.VMEM((2, 2, rows, n_cols), f32),
                pltpu.VMEM((2, hr, n_cols), f32), pltpu.VMEM((2, hr, n_cols), f32),
                pltpu.VMEM((hr, n_cols), f32), pltpu.VMEM((hr, n_cols), f32),
                pltpu.VMEM((2, 2, rows, nj), f32),
                pltpu.VMEM((2, hr, nj), f32), pltpu.VMEM((2, hr, nj), f32),
                pltpu.VMEM((hr, nj), f32), pltpu.VMEM((hr, nj), f32),
                pltpu.VMEM((rows, nj), bf16),
                pltpu.VMEM((rows, n_cols), bf16),
                dma((2,)), dma,
                dma((6,)), dma((6,)), dma((4,)), dma((4,)),
                dma((3, n)), dma((3, n)),
                dma((3, n)), dma((3, n)),
                dma((n,)), dma((n,)),
                dma((2, n + JOBS)), dma((2, n + JOBS)),
                dma((2, n + JOBS)), dma((2, n + JOBS)),
                dma((JOBS,)), dma((JOBS,)),
                dma((n,)),
            ],
            compiler_params=pltpu.CompilerParams(collective_id=0, has_side_effects=True, vmem_limit_bytes=62 * 2**20),
            name="product",
        )(a_rows, b_rows)

    return jax.shard_map(device_block, mesh=mesh, in_specs=(P(all_axes, None), P(all_axes, None)), out_specs=P(all_axes, None), check_vma=False)
```

time: 181 us -> 155 us (0.86)
  Pallas kernels: 178 us -> 152 us
    pallas_call x1, Pallas kernels: 178 us -> 152 us  [device_block(): pl.pallas_call(functools.partial(kernel, n_cols), out_shape=jax.ShapeDtyp...]
where the time goes in v2:
time: 155 us; the launch traced here: 154 us
  Pallas kernels  152 us (98%)
  local copies, waits for them, and re-layouts  2.36 us (2%)
    pallas_call x1, Pallas kernels, device_block(): pl.pallas_call(functools.partial(kernel, n_cols), out_shape=jax.ShapeDtyp...  152 us

profile of v2, /device:TPU:0, one launch (start us, length us, event | category | flops | bytes accessed | tf_op | source)
XLA Modules:
  0.0 154.2 jit_solution(7795008027254651175)
XLA Ops:
  0.0 151.8 %product.1 = bf16[128,4608]{1,0:T(8,128)(2,1)} custom-call(bf16[128,8192]{1,0:T(8,128)(2,1)} %a_ref.1, bf16[256,4608]{1,0:T(8,128)(2,1)} %b_ref.1), custom_call_target="tpu_custom_call" | custom-call | tf_op jit(solution)/shard_map/product/pallas_call | solution.py:347
  151.9 2.4 %copy.4 = bf16[128,4608]{1,0:T(8,128)(2,1)} copy(bf16[128,4608]{1,0:T(8,128)(2,1)} %product.1) | data formatting | bytes 2359296

commit v3 on v0

v3 whole, which is shorter than its diff:
```python
import functools

import jax
import jax.numpy as jnp
from jax import lax
from jax.experimental import pallas as pl
from jax.experimental.pallas import tpu as pltpu
from jax.sharding import PartitionSpec as P

MESH = pl.DeviceIdType.MESH
NC = 256
SHARED = 5
JOBS = 4
FIRST_JOB, JOB_PERIOD = 4, 3
AHEAD = 3
AHEAD_END = 5
A2_FIRST = 3
A2_STEPS = {5: 4, 7: 5, 9: 6, 11: 7}
LAG_MULTIPLY, LAG_MIDDLE, LAG_FINISH = 1, 1, 2
LAG_JOB_MIDDLE, LAG_JOB_FINISH = 2, 4
RING_Z, RING = 8, 4


def kernel(
    n_cols, a_ref, b_ref, c_ref,
    abuf, abuf2, bbuf, pbuf, rx, ry, sx, sy, pbuf2, rx2, ry2, sx2, sy2, cbuf, obuf,
    loc, a_rcv, a2_rcv, up0_rcv, dn0_rcv, out_rcv, up_rcv, dn_rcv, t_rcv, r_rcv, q_rcv, rj_rcv, qj_rcv, c_rcv,
    a_snd, a2_snd, up_snd, dn_snd, t_snd, r_snd, q_snd, rj_snd, qj_snd, c_snd, o_sem,
):
    depth, y, z = lax.axis_index("depth"), lax.axis_index("row"), lax.axis_index("col")
    x, core = depth // 2, depth % 2
    n_chunks = n_cols // NC
    rows_a = a_ref.shape[0]
    rows_b = b_ref.shape[0]
    half = 4 * rows_b
    hr = rows_a // 2
    jr = rows_a // JOBS
    f32 = jnp.float32
    wide = SHARED * NC

    inner = (z == 1) | (z == 2)
    end = (z == 0) | (z == 3)
    up = (z + 1, y, depth)
    down = (z - 1, y, depth)
    partner = (z + 1 - 2 * (z % 2), y, depth)
    twin = (z, y, 2 * x + 1 - core)
    x_peer = (z, y, 2 * (1 - x) + core)
    y_peer = (z, 1 - y, depth)
    diag = (z, 1 - y, 2 * (1 - x) + core)
    plane = (x_peer, y_peer, diag)
    plane_xy = ((1 - x, y), (x, 1 - y), (1 - x, 1 - y))

    def cols(j):
        return pl.ds(pl.multiple_of(j * NC, NC), NC)

    all_cols = pl.ds(0, n_cols)
    rest_cols = pl.ds(wide, n_cols - wide)

    def shared(j):
        return j < SHARED

    def works(j):
        return inner | ~shared(j)

    def when(*conds):
        both = conds[0]
        for c in conds[1:]:
            both = both & c
        return pl.when(both)

    def b_rows(src):
        return pl.ds(pl.multiple_of(core * half + src * rows_b, rows_b), rows_b)

    def a_cols(px, py, k):
        return pl.ds(pl.multiple_of(((2 * px + k) * 2 + py) * half, half), half)

    load_b = pltpu.make_async_copy(b_ref, bbuf.at[b_rows(z)], loc.at[0])
    load_b.start()
    load_a = []
    for k in range(2):
        load_a.append(pltpu.make_async_copy(a_ref.at[:, a_cols(x, y, k)], abuf.at[2 * x + y, :, pl.ds(k * half, half)], loc.at[1 + k]))
        load_a[-1].start()

    barrier = pltpu.get_barrier_semaphore()
    for peer in plane + (twin,):
        pl.semaphore_signal(barrier, inc=1, device_id=peer, device_id_type=MESH)

    @when(z < 3)
    def _():
        pl.semaphore_signal(barrier, inc=1, device_id=up, device_id_type=MESH)

    @when(z > 0)
    def _():
        pl.semaphore_signal(barrier, inc=1, device_id=down, device_id_type=MESH)

    @when(inner)
    def _():
        pl.semaphore_wait(barrier, 6)

    @when(end)
    def _():
        pl.semaphore_wait(barrier, 5)

    def remote(src, dst, snd, rcv, target):
        return pltpu.make_async_remote_copy(src, dst, snd, rcv, device_id=target, device_id_type=MESH)

    def await_sent(ref, sem):
        remote(ref, ref, sem, loc.at[0], twin).wait_send()

    def await_got(ref, sem):
        remote(ref, ref, loc.at[0], sem, twin).wait_recv()

    def a_copy(i, k):
        px, py = plane_xy[i]
        return remote(a_ref.at[:, a_cols(px, py, k)], abuf.at[2 * x + y, :, pl.ds(k * half, half)], a_snd.at[0], a_rcv.at[0], plane[i])

    def get_a():
        await_got(abuf.at[pl.ds(0, 3)], a_rcv.at[0])

    def job_rows(i):
        return pl.ds(pl.multiple_of(i * jr, jr), jr)

    def a2_copy(i):
        part = jr // 2
        rows = pl.ds(pl.multiple_of(i * part, part), part)
        return remote(abuf.at[:, rows], abuf2.at[:, rows], a2_snd.at[0], a2_rcv.at[i // 2], partner)

    def z_copy(j, src, snd, rcv, target):
        return remote(bbuf.at[b_rows(src), cols(j)], bbuf.at[b_rows(src), cols(j)], snd, rcv, target)

    def up_copy(h, j, src):
        return z_copy(j, src, up_snd.at[h], up0_rcv.at[j] if h == 0 else up_rcv.at[h - 1, j % RING_Z], up)

    def dn_copy(h, j, src):
        return z_copy(j, src, dn_snd.at[h], dn0_rcv.at[j] if h == 0 else dn_rcv.at[h - 1, j % RING_Z], down)

    def outward(src, snd, target):
        return remote(bbuf.at[b_rows(src), rest_cols], bbuf.at[b_rows(src), rest_cols], snd, out_rcv.at[0], target)

    def send_inward(j):
        @when(z < 2)
        def _():
            up_copy(0, j, z).start()

        @when(z > 1)
        def _():
            dn_copy(0, j, z).start()

    def relay(h, j):
        if h == 1:
            @when(inner)
            def _():
                up_copy(0, j, z - 1).wait_recv()

            @when(z == 3, j == SHARED)
            def _():
                outward(z - 1, up_snd.at[0], up).wait_recv()
        else:
            @when(z >= h, (z < 3) | ~shared(j))
            def _():
                up_copy(h - 1, j, z - h).wait_recv()

        if h < 3:
            @when(z >= h, (z < 2) | ((z == 2) & ~shared(j)))
            def _():
                up_copy(h, j, z - h).start()

        if h == 1:
            @when(inner)
            def _():
                dn_copy(0, j, z + 1).wait_recv()

            @when(z == 0, j == SHARED)
            def _():
                outward(z + 1, dn_snd.at[0], down).wait_recv()
        else:
            @when(z <= 3 - h, (z > 0) | ~shared(j))
            def _():
                dn_copy(h - 1, j, z + h).wait_recv()

        if h < 3:
            @when(z <= 3 - h, (z > 1) | ((z == 1) & ~shared(j)))
            def _():
                dn_copy(h, j, z + h).start()

    def twin_copy(j, who):
        rows = pl.ds(pl.multiple_of(who * half, half), half)
        return remote(bbuf.at[rows, cols(j)], bbuf.at[rows, cols(j)], t_snd.at[0], t_rcv.at[j % RING], twin)

    def send_twin(j):
        @when(works(j))
        def _():
            twin_copy(j, core).start()

    def view(own, j):
        if own:
            return pbuf, (rx, ry), (sx, sy), pl.ds(0, hr), pl.ds(hr, hr), pl.ds(0, hr), cols(j)
        lo = pl.multiple_of(j * jr, jr)
        return pbuf2, (rx2, ry2), (sx2, sy2), pl.ds(lo, jr // 2), pl.ds(pl.multiple_of(lo + jr // 2, jr // 2), jr // 2), pl.ds(pl.multiple_of(j * (jr // 2), jr // 2), jr // 2), pl.ds(0, wide)

    def sems(own, j):
        if own:
            return r_snd.at[0], r_rcv.at[j % RING], q_snd.at[0], q_rcv.at[j % RING]
        return rj_snd.at[0], rj_rcv.at[j], qj_snd.at[0], qj_rcv.at[j]

    def first_stage(own, j):
        p, (bx, by), _, low, high, rs, cs = view(own, j)
        snd, rcv, _, _ = sems(own, j)
        remote(p.at[1 - x, :, low, cs], bx.at[:, rs, cs], snd, rcv, x_peer).start()
        remote(p.at[:, 1 - y, high, cs], by.at[:, rs, cs], snd, rcv, y_peer).start()

    def middle(own, j):
        p, (bx, by), (qx, qy), low, high, rs, cs = view(own, j)
        _, got, snd, rcv = sems(own, j)
        await_got(p.at[:, :, low, cs], got)
        p[x, 1 - y, low, cs] += bx[1 - y, rs, cs]
        p[1 - x, y, high, cs] += by[1 - x, rs, cs]
        remote(p.at[x, 1 - y, low, cs], qy.at[rs, cs], snd, rcv, y_peer).start()
        remote(p.at[1 - x, y, high, cs], qx.at[rs, cs], snd, rcv, x_peer).start()

    def finish(own, j):
        p, (bx, by), (qx, qy), low, high, rs, cs = view(own, j)
        out = obuf if own else cbuf
        await_got(p.at[0, :, low, cs], sems(own, j)[3])
        top = p[x, y, low, cs] + bx[y, rs, cs] + qy[rs, cs]
        bottom = p[x, y, high, cs] + by[x, rs, cs] + qx[rs, cs]
        rows = pl.ds(0, rows_a) if own else job_rows(j)
        out[rows, cs] = jnp.concatenate([top, bottom], axis=0).astype(out.dtype)

    def o_copy(cs):
        return pltpu.make_async_copy(obuf.at[:, cs], c_ref.at[:, cs], o_sem.at[0])

    def c_copy(i):
        return remote(cbuf.at[job_rows(i)], obuf.at[job_rows(i), pl.ds(0, wide)], c_snd.at[0], c_rcv.at[0], partner)

    def multiply(j):
        when(inner, j == 0)(get_a)

        @when(works(j))
        def _():
            twin_copy(j, 1 - core).wait_recv()
            a = abuf[...].reshape(4 * rows_a, 2 * half)
            pbuf[:, :, :, cols(j)] = jnp.dot(a, bbuf[:, cols(j)], preferred_element_type=f32).reshape(2, 2, rows_a, NC)
            first_stage(True, j)

    def own_middle(j):
        when(works(j))(lambda: middle(True, j))

    def own_finish(j):
        @when(works(j))
        def _():
            finish(True, j)
            o_copy(cols(j)).start()

    def job_multiply(i):
        await_got(abuf2.at[:, job_rows(i)], a2_rcv.at[i])
        a = abuf2[:, job_rows(i), :].reshape(4 * jr, 2 * half)

        @pl.loop(0, wide // 256)
        def _(j):
            cs = pl.ds(pl.multiple_of(j * 256, 256), 256)
            pbuf2[:, :, job_rows(i), cs] = jnp.dot(a, bbuf[:, cs], preferred_element_type=f32).reshape(2, 2, jr, 256)

        first_stage(False, i)

    def job_middle(i):
        middle(False, i)

    def job_finish(i):
        finish(False, i)
        c_copy(i).start()

    def second_hop(j):
        relay(2, j)
        send_twin(j)

    def third_hop(j):
        relay(3, j)
        send_twin(j)

    def in_range(j, count, fn, *more):
        when((j >= 0) & (j < count), *more)(lambda: fn(j))

    def job(m, fn):
        m = m - FIRST_JOB
        when(inner, m >= 0, m % JOB_PERIOD == 0, m < JOBS * JOB_PERIOD)(lambda: fn(m // JOB_PERIOD))

    load_b.wait()

    @when(inner)
    def _():
        for j in range(AHEAD):
            send_inward(j)

    @when(end)
    def _():
        @pl.loop(0, AHEAD_END)
        def _(j):
            send_inward(j)

    @when(z == 2)
    def _():
        outward(z, up_snd.at[0], up).start()

    @when(z == 1)
    def _():
        outward(z, dn_snd.at[0], down).start()

    for i in range(3):
        for k in range(2):
            a_copy(i, k).start()
    for k in range(2):
        load_a[k].wait()

    @pl.loop(0, n_chunks + 2 + LAG_MULTIPLY + LAG_FINISH)
    def _(t):
        m = t - 2 - LAG_MULTIPLY + (z % 3 + 1) // 2

        @when(end, t == A2_FIRST)
        def _():
            get_a()
            for i in range(4):
                a2_copy(i).start()

        in_range(t + AHEAD, n_chunks, send_inward, inner)
        in_range(t + AHEAD_END, n_chunks, send_inward, end)
        for step, piece in A2_STEPS.items():
            @when(end, t == step)
            def _():
                a2_copy(piece).start()
        in_range(t, n_chunks, functools.partial(relay, 1))
        in_range(t - 1, n_chunks, functools.partial(relay, 2), end)
        in_range(m, n_chunks, multiply)
        job(m, job_multiply)
        in_range(m - LAG_MIDDLE, n_chunks, own_middle)
        job(m - LAG_JOB_MIDDLE, job_middle)
        in_range(m - LAG_FINISH, n_chunks, own_finish)
        job(m - LAG_JOB_FINISH, job_finish)
        in_range(t - 1, n_chunks, second_hop, inner)
        in_range(t - 2, n_chunks, third_hop, end)

    await_sent(abuf.at[pl.ds(0, 3)], a_snd.at[0])

    def sent(cs):
        await_sent(bbuf.at[pl.ds(0, half), cs], t_snd.at[0])
        await_sent(pbuf.at[:, :, pl.ds(0, hr), cs], r_snd.at[0])
        await_sent(pbuf.at[0, :, pl.ds(0, hr), cs], q_snd.at[0])

    def strip(cs):
        return bbuf.at[pl.ds(0, rows_b), cs]

    @when(inner)
    def _():
        sent(all_cols)
        await_sent(pbuf2.at[:, :, pl.ds(0, hr)], rj_snd.at[0])
        await_sent(pbuf2.at[0, :, pl.ds(0, hr)], qj_snd.at[0])
        await_sent(cbuf, c_snd.at[0])

    @when(z == 0)
    def _():
        await_sent(strip(all_cols), up_snd.at[0])

    @when(z == 3)
    def _():
        await_sent(strip(all_cols), dn_snd.at[0])

    @when(z == 1)
    def _():
        for h in range(2):
            await_sent(strip(all_cols), up_snd.at[h])
        for h in range(3):
            await_sent(strip(rest_cols), dn_snd.at[h])

    @when(z == 2)
    def _():
        for h in range(2):
            await_sent(strip(all_cols), dn_snd.at[h])
        for h in range(3):
            await_sent(strip(rest_cols), up_snd.at[h])

    @when(end)
    def _():
        sent(rest_cols)
        await_sent(abuf, a2_snd.at[0])
        await_got(cbuf, c_rcv.at[0])
        o_copy(pl.ds(0, wide)).start()

    o_copy(all_cols).wait()


def solution(mesh):
    all_axes = ("depth", "row", "col")

    def device_block(a_rows, b_rows):
        rows, depth = a_rows.shape
        rows_b, n_cols = b_rows.shape
        n = n_cols // NC
        hr = rows // 2
        nj = SHARED * NC
        dma = pltpu.SemaphoreType.DMA
        bf16, f32 = jnp.bfloat16, jnp.float32
        return pl.pallas_call(
            functools.partial(kernel, n_cols),
            out_shape=jax.ShapeDtypeStruct((rows, n_cols), bf16),
            in_specs=[pl.BlockSpec(memory_space=pl.ANY)] * 2,
            out_specs=pl.BlockSpec(memory_space=pl.ANY),
            scratch_shapes=[
                pltpu.VMEM((4, rows, 8 * rows_b), bf16),
                pltpu.VMEM((4, rows, 8 * rows_b), bf16),
                pltpu.VMEM((8 * rows_b, n_cols), bf16),
                pltpu.VMEM((2, 2, rows, n_cols), f32),
                pltpu.VMEM((2, hr, n_cols), f32), pltpu.VMEM((2, hr, n_cols), f32),
                pltpu.VMEM((hr, n_cols), f32), pltpu.VMEM((hr, n_cols), f32),
                pltpu.VMEM((2, 2, rows, nj), f32),
                pltpu.VMEM((2, hr, nj), f32), pltpu.VMEM((2, hr, nj), f32),
                pltpu.VMEM((hr, nj), f32), pltpu.VMEM((hr, nj), f32),
                pltpu.VMEM((rows, nj), bf16),
                pltpu.VMEM((rows, n_cols), bf16),
                dma((3,)), dma((1,)), dma((JOBS,)),
                dma((n,)), dma((n,)), dma((1,)), dma((2, RING_Z)), dma((2, RING_Z)),
                dma((RING,)), dma((RING,)), dma((RING,)), dma((JOBS,)), dma((JOBS,)), dma((1,)),
                dma((1,)), dma((1,)), dma((3,)), dma((3,)),
                dma((1,)), dma((1,)), dma((1,)), dma((1,)), dma((1,)), dma((1,)), dma((1,)),
            ],
            compiler_params=pltpu.CompilerParams(collective_id=0, has_side_effects=True, vmem_limit_bytes=62 * 2**20),
            name="product",
        )(a_rows, b_rows)

    return jax.shard_map(device_block, mesh=mesh, in_specs=(P(all_axes, None), P(all_axes, None)), out_specs=P(all_axes, None), check_vma=False)
```

time: 421 us -> 143 us (0.34)
  waiting for transfers between devices: 253 us -> 0 us
  Pallas kernels: 0 us -> 140 us
  blocking collectives: 122 us -> 0 us
  matrix products: 16.3 us -> 0 us
  between operations: 13.1 us -> 0.01 us
  local copies, waits for them, and re-layouts: 14.5 us -> 2.36 us
    all_gather x2 -> x0, waiting for transfers between devices: 178 us -> none  [the longest x1 151 us: device_block(): a_block = lax.all_gather(a_part, 'col', axis=0, tiled=True)]
    pallas_call x0 -> x1, Pallas kernels: none -> 140 us  [device_block(): pl.pallas_call(functools.partial(kernel, n_cols), out_shape=jax.ShapeDtyp...]
    all_to_all x3 -> x0, blocking collectives: 122 us -> none  [the longest x1 60 us: device_block(): b_part = lax.all_to_all(b_rows, 'col', 1, 0, tiled=True)]
    reduce_scatter x1 -> x0, waiting for transfers between devices: 75.6 us -> none  [device_block(): summed = lax.psum_scatter(grouped, 'depth', scatter_dimension=1, tiled=True)]
    dot_general x1 -> x0, matrix products: 16.3 us -> none  [device_block(): part_sum = jnp.dot(a_block, b_block, preferred_element_type=jnp.float32)]
    all_to_all x3 -> x0, local copies, waits for them, and re-layouts: 6.33 us -> none  [the longest x1 2.69 us: device_block(): a_part = lax.all_to_all(a_rows, 'depth', 1, 0, tiled=True)]
    unnamed x4 -> x1, local copies, waits for them, and re-layouts: 8.22 us -> 2.36 us
  transfers between devices with their start and end apart: 3 -> 0, of which waited for: 3 -> 0; matrix products, arithmetic and copies ran while one was open for 1% -> 0% of each run, Pallas kernels for 0% -> 0%
where the time goes in v3:
time: 143 us
  Pallas kernels  140 us (98%)
  local copies, waits for them, and re-layouts  2.36 us (2%)
    pallas_call x1, Pallas kernels, device_block(): pl.pallas_call(functools.partial(kernel, n_cols), out_shape=jax.ShapeDtyp...  140 us

profile of v3, /device:TPU:0, one launch (start us, length us, event | category | flops | bytes accessed | tf_op | source)
XLA Modules:
  0.0 142.9 jit_solution(18226080327008525426)
XLA Ops:
  0.0 140.5 %product.1 = bf16[128,4608]{1,0:T(8,128)(2,1)} custom-call(bf16[128,8192]{1,0:T(8,128)(2,1)} %a_ref.1, bf16[256,4608]{1,0:T(8,128)(2,1)} %b_ref.1), custom_call_target="tpu_custom_call" | custom-call | tf_op jit(solution)/shard_map/product/pallas_call | solution.py:402
  140.5 2.4 %copy.4 = bf16[128,4608]{1,0:T(8,128)(2,1)} copy(bf16[128,4608]{1,0:T(8,128)(2,1)} %product.1) | data formatting | bytes 2359296

commit v4 on v3

--- a/solution.py
+++ b/solution.py
@@ -16,16 +16,18 @@
 AHEAD_END = 5
 A2_FIRST = 3
 A2_STEPS = {5: 4, 7: 5, 9: 6, 11: 7}
-LAG_MULTIPLY, LAG_MIDDLE, LAG_FINISH = 1, 1, 2
+LAG_MULTIPLY = 1
+LAG_MIDDLE, LAG_FINISH = (1, 1), (3, 2)
 LAG_JOB_MIDDLE, LAG_JOB_FINISH = 2, 4
-RING_Z, RING = 8, 4
+RING_Z, RING = 12, 8
+EXTRA = (9, 12)
 
 
 def kernel(
     n_cols, a_ref, b_ref, c_ref,
-    abuf, abuf2, bbuf, pbuf, rx, ry, sx, sy, pbuf2, rx2, ry2, sx2, sy2, cbuf, obuf,
+    abuf, abuf2, bbuf, pbuf, rx, ry, sx, sy, pbuf2, rx2, ry2, sx2, sy2, cbuf,
     loc, a_rcv, a2_rcv, up0_rcv, dn0_rcv, out_rcv, up_rcv, dn_rcv, t_rcv, r_rcv, q_rcv, rj_rcv, qj_rcv, c_rcv,
-    a_snd, a2_snd, up_snd, dn_snd, t_snd, r_snd, q_snd, rj_snd, qj_snd, c_snd, o_sem,
+    a_snd, a2_snd, up_snd, dn_snd, t_snd, r_snd, q_snd, rj_snd, qj_snd, c_snd,
 ):
     depth, y, z = lax.axis_index("depth"), lax.axis_index("row"), lax.axis_index("col")
     x, core = depth // 2, depth % 2
@@ -220,18 +222,15 @@
 
     def finish(own, j):
         p, (bx, by), (qx, qy), low, high, rs, cs = view(own, j)
-        out = obuf if own else cbuf
+        out = c_ref if own else cbuf
         await_got(p.at[0, :, low, cs], sems(own, j)[3])
         top = p[x, y, low, cs] + bx[y, rs, cs] + qy[rs, cs]
         bottom = p[x, y, high, cs] + by[x, rs, cs] + qx[rs, cs]
         rows = pl.ds(0, rows_a) if own else job_rows(j)
         out[rows, cs] = jnp.concatenate([top, bottom], axis=0).astype(out.dtype)
 
-    def o_copy(cs):
-        return pltpu.make_async_copy(obuf.at[:, cs], c_ref.at[:, cs], o_sem.at[0])
-
     def c_copy(i):
-        return remote(cbuf.at[job_rows(i)], obuf.at[job_rows(i), pl.ds(0, wide)], c_snd.at[0], c_rcv.at[0], partner)
+        return remote(cbuf.at[job_rows(i)], c_ref.at[job_rows(i), pl.ds(0, wide)], c_snd.at[0], c_rcv.at[0], partner)
 
     def multiply(j):
         when(inner, j == 0)(get_a)
@@ -250,7 +249,6 @@
         @when(works(j))
         def _():
             finish(True, j)
-            o_copy(cols(j)).start()
 
     def job_multiply(i):
         await_got(abuf2.at[:, job_rows(i)], a2_rcv.at[i])
@@ -312,9 +310,31 @@
     for k in range(2):
         load_a[k].wait()
 
-    @pl.loop(0, n_chunks + 2 + LAG_MULTIPLY + LAG_FINISH)
+    flag = (z % 3 + 1) // 2
+
+    def first_hops(r):
+        in_range(r + AHEAD, n_chunks, send_inward, inner)
+        in_range(r + AHEAD_END, n_chunks, send_inward, end)
+        for step, piece in A2_STEPS.items():
+            @when(end, r == step)
+            def _():
+                a2_copy(piece).start()
+        in_range(r, n_chunks, functools.partial(relay, 1))
+        in_range(r - 1, n_chunks, functools.partial(relay, 2), end)
+
+    def last_hops(r):
+        in_range(r - 1, n_chunks, second_hop, inner)
+        in_range(r - 2, n_chunks, third_hop, end)
+
+    def lag(pair):
+        return pair[1] + flag * (pair[0] - pair[1])
+
+    @pl.loop(0, n_chunks + 2 + LAG_MULTIPLY + max(LAG_FINISH))
     def _(t):
-        m = t - 2 - LAG_MULTIPLY + (z % 3 + 1) // 2
+        m = t - 2 - LAG_MULTIPLY + flag
+        r = t
+        for e in EXTRA:
+            r = r + flag * jnp.where(t > e, 1, 0)
 
         @when(end, t == A2_FIRST)
         def _():
@@ -322,22 +342,23 @@
             for i in range(4):
                 a2_copy(i).start()
 
-        in_range(t + AHEAD, n_chunks, send_inward, inner)
-        in_range(t + AHEAD_END, n_chunks, send_inward, end)
-        for step, piece in A2_STEPS.items():
-            @when(end, t == step)
-            def _():
-                a2_copy(piece).start()
-        in_range(t, n_chunks, functools.partial(relay, 1))
-        in_range(t - 1, n_chunks, functools.partial(relay, 2), end)
+        first_hops(r)
         in_range(m, n_chunks, multiply)
         job(m, job_multiply)
-        in_range(m - LAG_MIDDLE, n_chunks, own_middle)
+        in_range(m - lag(LAG_MIDDLE), n_chunks, own_middle)
         job(m - LAG_JOB_MIDDLE, job_middle)
-        in_range(m - LAG_FINISH, n_chunks, own_finish)
+        in_range(m - lag(LAG_FINISH), n_chunks, own_finish)
         job(m - LAG_JOB_FINISH, job_finish)
-        in_range(t - 1, n_chunks, second_hop, inner)
-        in_range(t - 2, n_chunks, third_hop, end)
+        last_hops(r)
+
+        extra = t == EXTRA[0]
+        for e in EXTRA[1:]:
+            extra = extra | (t == e)
+
+        @when(inner, extra)
+        def _():
+            first_hops(r + 1)
+            last_hops(r + 1)
 
     await_sent(abuf.at[pl.ds(0, 3)], a_snd.at[0])
 
@@ -383,9 +404,6 @@
         sent(rest_cols)
         await_sent(abuf, a2_snd.at[0])
         await_got(cbuf, c_rcv.at[0])
-        o_copy(pl.ds(0, wide)).start()
-
-    o_copy(all_cols).wait()
 
 
 def solution(mesh):
@@ -401,9 +419,9 @@
         bf16, f32 = jnp.bfloat16, jnp.float32
         return pl.pallas_call(
             functools.partial(kernel, n_cols),
-            out_shape=jax.ShapeDtypeStruct((rows, n_cols), bf16),
+            out_shape=pltpu.VMEM((rows, n_cols), bf16),
             in_specs=[pl.BlockSpec(memory_space=pl.ANY)] * 2,
-            out_specs=pl.BlockSpec(memory_space=pl.ANY),
+            out_specs=pl.BlockSpec(memory_space=pltpu.VMEM),
             scratch_shapes=[
                 pltpu.VMEM((4, rows, 8 * rows_b), bf16),
                 pltpu.VMEM((4, rows, 8 * rows_b), bf16),
@@ -415,14 +433,13 @@
                 pltpu.VMEM((2, hr, nj), f32), pltpu.VMEM((2, hr, nj), f32),
                 pltpu.VMEM((hr, nj), f32), pltpu.VMEM((hr, nj), f32),
                 pltpu.VMEM((rows, nj), bf16),
-                pltpu.VMEM((rows, n_cols), bf16),
                 dma((3,)), dma((1,)), dma((JOBS,)),
                 dma((n,)), dma((n,)), dma((1,)), dma((2, RING_Z)), dma((2, RING_Z)),
                 dma((RING,)), dma((RING,)), dma((RING,)), dma((JOBS,)), dma((JOBS,)), dma((1,)),
                 dma((1,)), dma((1,)), dma((3,)), dma((3,)),
-                dma((1,)), dma((1,)), dma((1,)), dma((1,)), dma((1,)), dma((1,)), dma((1,)),
+                dma((1,)), dma((1,)), dma((1,)), dma((1,)), dma((1,)), dma((1,)),
             ],
-            compiler_params=pltpu.CompilerParams(collective_id=0, has_side_effects=True, vmem_limit_bytes=62 * 2**20),
+            compiler_params=pltpu.CompilerParams(collective_id=0, has_side_effects=True, vmem_limit_bytes=56 * 2**20),
             name="product",
         )(a_rows, b_rows)
 

time: 143 us -> 138 us (0.965)
  Pallas kernels: 140 us -> 136 us
    pallas_call x1, Pallas kernels: 140 us -> 136 us  [device_block(): pl.pallas_call(functools.partial(kernel, n_cols), out_shape=pltpu.VMEM((r...]
where the time goes in v4:
time: 138 us; the launch traced here: 137 us
  Pallas kernels  136 us (99%)
    pallas_call x1, Pallas kernels, device_block(): pl.pallas_call(functools.partial(kernel, n_cols), out_shape=pltpu.VMEM((r...  136 us

profile of v4, /device:TPU:0, one launch (start us, length us, event | category | flops | bytes accessed | tf_op | source)
XLA Modules:
  0.0 137.4 jit_solution(2366540768616465434)
XLA Ops:
  0.0 136.3 %product.1 = bf16[128,4608]{1,0:T(8,128)(2,1)S(1)} custom-call(bf16[128,8192]{1,0:T(8,128)(2,1)} %a_ref.1, bf16[256,4608]{1,0:T(8,128)(2,1)} %b_ref.1), custom_call_target="tpu_custom_call" | custom-call | tf_op jit(solution)/shard_map/product/pallas_call | solution.py:420
  136.4 1.0 copy.4

commit v5 on v4

--- a/solution.py
+++ b/solution.py
@@ -12,7 +12,7 @@
 SHARED = 5
 JOBS = 4
 FIRST_JOB, JOB_PERIOD = 4, 3
-AHEAD = 3
+AHEAD = 2
 AHEAD_END = 5
 A2_FIRST = 3
 A2_STEPS = {5: 4, 7: 5, 9: 6, 11: 7}
@@ -20,7 +20,8 @@
 LAG_MIDDLE, LAG_FINISH = (1, 1), (3, 2)
 LAG_JOB_MIDDLE, LAG_JOB_FINISH = 2, 4
 RING_Z, RING = 12, 8
-EXTRA = (9, 12)
+EXTRA = (12,)
+BACK = 17
 
 
 def kernel(
@@ -266,7 +267,10 @@
 
     def job_finish(i):
         finish(False, i)
-        c_copy(i).start()
+
+        @when(i == JOBS - 1)
+        def _():
+            c_copy(i).start()
 
     def second_hop(j):
         relay(2, j)
@@ -283,6 +287,9 @@
         m = m - FIRST_JOB
         when(inner, m >= 0, m % JOB_PERIOD == 0, m < JOBS * JOB_PERIOD)(lambda: fn(m // JOB_PERIOD))
 
+    for i in range(3):
+        for k in range(2):
+            a_copy(i, k).start()
     load_b.wait()
 
     @when(inner)
@@ -304,9 +311,6 @@
     def _():
         outward(z, dn_snd.at[0], down).start()
 
-    for i in range(3):
-        for k in range(2):
-            a_copy(i, k).start()
     for k in range(2):
         load_a[k].wait()
 
@@ -350,6 +354,11 @@
         in_range(m - lag(LAG_FINISH), n_chunks, own_finish)
         job(m - LAG_JOB_FINISH, job_finish)
         last_hops(r)
+
+        @when(inner, t == BACK)
+        def _():
+            for i in range(JOBS - 1):
+                c_copy(i).start()
 
         extra = t == EXTRA[0]
         for e in EXTRA[1:]:

time: 138 us -> 133 us (0.964)
  Pallas kernels: 136 us -> 132 us
    pallas_call x1, Pallas kernels: 136 us -> 132 us  [device_block(): pl.pallas_call(functools.partial(kernel, n_cols), out_shape=pltpu.VMEM((r...]
where the time goes in v5:
time: 133 us
  Pallas kernels  132 us (99%)
    pallas_call x1, Pallas kernels, device_block(): pl.pallas_call(functools.partial(kernel, n_cols), out_shape=pltpu.VMEM((r...  132 us

profile of v5, /device:TPU:0, one launch (start us, length us, event | category | flops | bytes accessed | tf_op | source)
XLA Modules:
  0.0 133.2 jit_solution(9366471191607459475)
XLA Ops:
  0.0 132.1 %product.1 = bf16[128,4608]{1,0:T(8,128)(2,1)S(1)} custom-call(bf16[128,8192]{1,0:T(8,128)(2,1)} %a_ref.1, bf16[256,4608]{1,0:T(8,128)(2,1)} %b_ref.1), custom_call_target="tpu_custom_call" | custom-call | tf_op jit(solution)/shard_map/product/pallas_call | solution.py:429
  132.2 1.0 copy.4

commit v6 on v5

--- a/solution.py
+++ b/solution.py
@@ -1,3 +1,4 @@
+import collections
 import functools
 
 import jax
@@ -8,7 +9,8 @@
 from jax.sharding import PartitionSpec as P
 
 MESH = pl.DeviceIdType.MESH
-NC = 256
+NC, SMALL = 256, 128
+N_SMALL = 0
 SHARED = 5
 JOBS = 4
 FIRST_JOB, JOB_PERIOD = 4, 3
@@ -16,23 +18,30 @@
 AHEAD_END = 5
 A2_FIRST = 3
 A2_STEPS = {5: 4, 7: 5, 9: 6, 11: 7}
-LAG_MULTIPLY = 1
-LAG_MIDDLE, LAG_FINISH = (1, 1), (3, 2)
+LAG_MULTIPLY = (1, 1)
+LAG_MIDDLE, LAG_FINISH = (1, 1), (3, 3)
 LAG_JOB_MIDDLE, LAG_JOB_FINISH = 2, 4
 RING_Z, RING = 12, 8
 EXTRA = (12,)
 BACK = 17
 
+Chunk = collections.namedtuple("Chunk", "j start width")
+
+
+def n_big(n_cols):
+    return (n_cols - N_SMALL * SMALL) // NC
+
 
 def kernel(
     n_cols, a_ref, b_ref, c_ref,
     abuf, abuf2, bbuf, pbuf, rx, ry, sx, sy, pbuf2, rx2, ry2, sx2, sy2, cbuf,
-    loc, a_rcv, a2_rcv, up0_rcv, dn0_rcv, out_rcv, up_rcv, dn_rcv, t_rcv, r_rcv, q_rcv, rj_rcv, qj_rcv, c_rcv,
+    loc, a_rcv, a2_rcv, end_rcv, mid_rcv, out_rcv, hop_rcv, t_rcv, r_rcv, q_rcv, rj_rcv, qj_rcv, c_rcv,
     a_snd, a2_snd, up_snd, dn_snd, t_snd, r_snd, q_snd, rj_snd, qj_snd, c_snd,
 ):
     depth, y, z = lax.axis_index("depth"), lax.axis_index("row"), lax.axis_index("col")
     x, core = depth // 2, depth % 2
-    n_chunks = n_cols // NC
+    big = n_big(n_cols)
+    n_chunks = big + N_SMALL
     rows_a = a_ref.shape[0]
     rows_b = b_ref.shape[0]
     half = 4 * rows_b
@@ -53,8 +62,14 @@
     plane = (x_peer, y_peer, diag)
     plane_xy = ((1 - x, y), (x, 1 - y), (1 - x, 1 - y))
 
-    def cols(j):
-        return pl.ds(pl.multiple_of(j * NC, NC), NC)
+    def big_chunk(j):
+        return Chunk(j, j * NC, NC)
+
+    def small_chunk(j):
+        return Chunk(j, j * SMALL + big * (NC - SMALL), SMALL)
+
+    def cols(c):
+        return pl.ds(pl.multiple_of(c.start, c.width), c.width)
 
     all_cols = pl.ds(0, n_cols)
     rest_cols = pl.ds(wide, n_cols - wide)
@@ -62,8 +77,8 @@
     def shared(j):
         return j < SHARED
 
-    def works(j):
-        return inner | ~shared(j)
+    def works(c):
+        return inner | ~shared(c.j)
 
     def when(*conds):
         both = conds[0]
@@ -128,72 +143,106 @@
         rows = pl.ds(pl.multiple_of(i * part, part), part)
         return remote(abuf.at[:, rows], abuf2.at[:, rows], a2_snd.at[0], a2_rcv.at[i // 2], partner)
 
-    def z_copy(j, src, snd, rcv, target):
-        return remote(bbuf.at[b_rows(src), cols(j)], bbuf.at[b_rows(src), cols(j)], snd, rcv, target)
-
-    def up_copy(h, j, src):
-        return z_copy(j, src, up_snd.at[h], up0_rcv.at[j] if h == 0 else up_rcv.at[h - 1, j % RING_Z], up)
-
-    def dn_copy(h, j, src):
-        return z_copy(j, src, dn_snd.at[h], dn0_rcv.at[j] if h == 0 else dn_rcv.at[h - 1, j % RING_Z], down)
+    def z_copy(c, src, snd, rcv, target):
+        return remote(bbuf.at[b_rows(src), cols(c)], bbuf.at[b_rows(src), cols(c)], snd, rcv, target)
+
+    def up_copy(h, c, src, rcv=None):
+        return z_copy(c, src, up_snd.at[h], hop_rcv.at[h - 1, c.j % RING_Z] if rcv is None else rcv, up)
+
+    def dn_copy(h, c, src, rcv=None):
+        return z_copy(c, src, dn_snd.at[h], hop_rcv.at[h - 1, c.j % RING_Z] if rcv is None else rcv, down)
 
     def outward(src, snd, target):
         return remote(bbuf.at[b_rows(src), rest_cols], bbuf.at[b_rows(src), rest_cols], snd, out_rcv.at[0], target)
 
-    def send_inward(j):
-        @when(z < 2)
-        def _():
-            up_copy(0, j, z).start()
-
-        @when(z > 1)
-        def _():
-            dn_copy(0, j, z).start()
-
-    def relay(h, j):
-        if h == 1:
-            @when(inner)
-            def _():
-                up_copy(0, j, z - 1).wait_recv()
-
-            @when(z == 3, j == SHARED)
-            def _():
-                outward(z - 1, up_snd.at[0], up).wait_recv()
-        else:
-            @when(z >= h, (z < 3) | ~shared(j))
-            def _():
-                up_copy(h - 1, j, z - h).wait_recv()
-
-        if h < 3:
-            @when(z >= h, (z < 2) | ((z == 2) & ~shared(j)))
-            def _():
-                up_copy(h, j, z - h).start()
-
-        if h == 1:
-            @when(inner)
-            def _():
-                dn_copy(0, j, z + 1).wait_recv()
-
-            @when(z == 0, j == SHARED)
-            def _():
-                outward(z + 1, dn_snd.at[0], down).wait_recv()
-        else:
-            @when(z <= 3 - h, (z > 0) | ~shared(j))
-            def _():
-                dn_copy(h - 1, j, z + h).wait_recv()
-
-        if h < 3:
-            @when(z <= 3 - h, (z > 1) | ((z == 1) & ~shared(j)))
-            def _():
-                dn_copy(h, j, z + h).start()
-
-    def twin_copy(j, who):
-        rows = pl.ds(pl.multiple_of(who * half, half), half)
-        return remote(bbuf.at[rows, cols(j)], bbuf.at[rows, cols(j)], t_snd.at[0], t_rcv.at[j % RING], twin)
-
-    def send_twin(j):
-        @when(works(j))
-        def _():
-            twin_copy(j, core).start()
+    def send_inward(c):
+        @when(z == 0)
+        def _():
+            up_copy(0, c, z, end_rcv.at[c.j]).start()
+
+        @when(z == 1)
+        def _():
+            up_copy(0, c, z, mid_rcv.at[c.j % RING_Z]).start()
+
+        @when(z == 2)
+        def _():
+            dn_copy(0, c, z, mid_rcv.at[c.j % RING_Z]).start()
+
+        @when(z == 3)
+        def _():
+            dn_copy(0, c, z, end_rcv.at[c.j]).start()
+
+    def first_hop(c):
+        @when(z == 1)
+        def _():
+            dn_copy(0, c, z + 1, mid_rcv.at[c.j % RING_Z]).wait_recv()
+            when(~shared(c.j))(lambda: dn_copy(1, c, z + 1).start())
+            up_copy(0, c, z - 1, end_rcv.at[c.j]).wait_recv()
+            up_copy(1, c, z - 1).start()
+
+        @when(z == 2)
+        def _():
+            up_copy(0, c, z - 1, mid_rcv.at[c.j % RING_Z]).wait_recv()
+            when(~shared(c.j))(lambda: up_copy(1, c, z - 1).start())
+            dn_copy(0, c, z + 1, end_rcv.at[c.j]).wait_recv()
+            dn_copy(1, c, z + 1).start()
+
+        @when(z == 3, c.j == SHARED)
+        def _():
+            outward(z - 1, up_snd.at[0], up).wait_recv()
+
+        @when(z == 0, c.j == SHARED)
+        def _():
+            outward(z + 1, dn_snd.at[0], down).wait_recv()
+
+        when(inner)(lambda: twin_first(c))
+
+    def second_hop(c):
+        @when(z == 1)
+        def _():
+            dn_copy(1, c, z + 2).wait_recv()
+            when(~shared(c.j))(lambda: dn_copy(2, c, z + 2).start())
+
+        @when(z == 2)
+        def _():
+            up_copy(1, c, z - 2).wait_recv()
+            when(~shared(c.j))(lambda: up_copy(2, c, z - 2).start())
+
+        when(inner)(lambda: twin_last(c))
+
+        @when(z == 3, ~shared(c.j))
+        def _():
+            up_copy(1, c, z - 2).wait_recv()
+            twin_first(c)
+
+        @when(z == 0, ~shared(c.j))
+        def _():
+            dn_copy(1, c, z + 2).wait_recv()
+            twin_first(c)
+
+    def third_hop(c):
+        @when(z == 3, ~shared(c.j))
+        def _():
+            up_copy(2, c, z - 3).wait_recv()
+            twin_last(c)
+
+        @when(z == 0, ~shared(c.j))
+        def _():
+            dn_copy(2, c, z + 3).wait_recv()
+            twin_last(c)
+
+    def twin_part(c, who, start, rows):
+        at = pl.ds(pl.multiple_of(who * half + start, rows_b), rows)
+        return remote(bbuf.at[at, cols(c)], bbuf.at[at, cols(c)], t_snd.at[0], t_rcv.at[c.j % RING], twin)
+
+    def twin_first(c):
+        twin_part(c, core, z // 2 * rows_b, 3 * rows_b).start()
+
+    def twin_last(c):
+        twin_part(c, core, (1 - z // 2) * 3 * rows_b, rows_b).start()
+
+    def get_twin(c):
+        twin_part(c, 1 - core, 0, half).wait_recv()
 
     def view(own, j):
         if own:
@@ -203,7 +252,7 @@
 
     def sems(own, j):
         if own:
-            return r_snd.at[0], r_rcv.at[j % RING], q_snd.at[0], q_rcv.at[j % RING]
+            return r_snd.at[0], r_rcv.at[j.j % RING], q_snd.at[0], q_rcv.at[j.j % RING]
         return rj_snd.at[0], rj_rcv.at[j], qj_snd.at[0], qj_rcv.at[j]
 
     def first_stage(own, j):
@@ -233,23 +282,23 @@
     def c_copy(i):
         return remote(cbuf.at[job_rows(i)], c_ref.at[job_rows(i), pl.ds(0, wide)], c_snd.at[0], c_rcv.at[0], partner)
 
-    def multiply(j):
-        when(inner, j == 0)(get_a)
-
-        @when(works(j))
-        def _():
-            twin_copy(j, 1 - core).wait_recv()
+    def multiply(c):
+        when(inner, c.j == 0)(get_a)
+
+        @when(works(c))
+        def _():
+            get_twin(c)
             a = abuf[...].reshape(4 * rows_a, 2 * half)
-            pbuf[:, :, :, cols(j)] = jnp.dot(a, bbuf[:, cols(j)], preferred_element_type=f32).reshape(2, 2, rows_a, NC)
-            first_stage(True, j)
-
-    def own_middle(j):
-        when(works(j))(lambda: middle(True, j))
-
-    def own_finish(j):
-        @when(works(j))
-        def _():
-            finish(True, j)
+            pbuf[:, :, :, cols(c)] = jnp.dot(a, bbuf[:, cols(c)], preferred_element_type=f32).reshape(2, 2, rows_a, c.width)
+            first_stage(True, c)
+
+    def own_middle(c):
+        when(works(c))(lambda: middle(True, c))
+
+    def own_finish(c):
+        @when(works(c))
+        def _():
+            finish(True, c)
 
     def job_multiply(i):
         await_got(abuf2.at[:, job_rows(i)], a2_rcv.at[i])
@@ -272,16 +321,9 @@
         def _():
             c_copy(i).start()
 
-    def second_hop(j):
-        relay(2, j)
-        send_twin(j)
-
-    def third_hop(j):
-        relay(3, j)
-        send_twin(j)
-
-    def in_range(j, count, fn, *more):
-        when((j >= 0) & (j < count), *more)(lambda: fn(j))
+    def in_range(j, fn, *more):
+        when((j >= 0) & (j < big), *more)(lambda: fn(big_chunk(j)))
+        when((j >= big) & (j < n_chunks), *more)(lambda: fn(small_chunk(j)))
 
     def job(m, fn):
         m = m - FIRST_JOB
@@ -295,13 +337,13 @@
     @when(inner)
     def _():
         for j in range(AHEAD):
-            send_inward(j)
+            send_inward(big_chunk(j))
 
     @when(end)
     def _():
         @pl.loop(0, AHEAD_END)
         def _(j):
-            send_inward(j)
+            send_inward(big_chunk(j))
 
     @when(z == 2)
     def _():
@@ -317,25 +359,25 @@
     flag = (z % 3 + 1) // 2
 
     def first_hops(r):
-        in_range(r + AHEAD, n_chunks, send_inward, inner)
-        in_range(r + AHEAD_END, n_chunks, send_inward, end)
+        in_range(r + AHEAD, send_inward, inner)
+        in_range(r + AHEAD_END, send_inward, end)
         for step, piece in A2_STEPS.items():
             @when(end, r == step)
             def _():
                 a2_copy(piece).start()
-        in_range(r, n_chunks, functools.partial(relay, 1))
-        in_range(r - 1, n_chunks, functools.partial(relay, 2), end)
+        in_range(r, first_hop)
+        in_range(r - 1, second_hop, end)
 
     def last_hops(r):
-        in_range(r - 1, n_chunks, second_hop, inner)
-        in_range(r - 2, n_chunks, third_hop, end)
+        in_range(r - 1, second_hop, inner)
+        in_range(r - 2, third_hop, end)
 
     def lag(pair):
         return pair[1] + flag * (pair[0] - pair[1])
 
-    @pl.loop(0, n_chunks + 2 + LAG_MULTIPLY + max(LAG_FINISH))
+    @pl.loop(0, n_chunks + 2 + max(LAG_MULTIPLY) + max(LAG_FINISH))
     def _(t):
-        m = t - 2 - LAG_MULTIPLY + flag
+        m = t - 2 - lag(LAG_MULTIPLY) + flag
         r = t
         for e in EXTRA:
             r = r + flag * jnp.where(t > e, 1, 0)
@@ -347,11 +389,11 @@
                 a2_copy(i).start()
 
         first_hops(r)
-        in_range(m, n_chunks, multiply)
+        in_range(m, multiply)
         job(m, job_multiply)
-        in_range(m - lag(LAG_MIDDLE), n_chunks, own_middle)
+        in_range(m - lag(LAG_MIDDLE), own_middle)
         job(m - LAG_JOB_MIDDLE, job_middle)
-        in_range(m - lag(LAG_FINISH), n_chunks, own_finish)
+        in_range(m - lag(LAG_FINISH), own_finish)
         job(m - LAG_JOB_FINISH, job_finish)
         last_hops(r)
 
@@ -421,7 +463,7 @@
     def device_block(a_rows, b_rows):
         rows, depth = a_rows.shape
         rows_b, n_cols = b_rows.shape
-        n = n_cols // NC
+        n = n_big(n_cols) + N_SMALL
         hr = rows // 2
         nj = SHARED * NC
         dma = pltpu.SemaphoreType.DMA
@@ -443,7 +485,7 @@
                 pltpu.VMEM((hr, nj), f32), pltpu.VMEM((hr, nj), f32),
                 pltpu.VMEM((rows, nj), bf16),
                 dma((3,)), dma((1,)), dma((JOBS,)),
-                dma((n,)), dma((n,)), dma((1,)), dma((2, RING_Z)), dma((2, RING_Z)),
+                dma((n,)), dma((RING_Z,)), dma((1,)), dma((2, RING_Z)),
                 dma((RING,)), dma((RING,)), dma((RING,)), dma((JOBS,)), dma((JOBS,)), dma((1,)),
                 dma((1,)), dma((1,)), dma((3,)), dma((3,)),
                 dma((1,)), dma((1,)), dma((1,)), dma((1,)), dma((1,)), dma((1,)),

time: 133 us -> 133 us (level)
  no operation moved by 1% of the time
where the time goes in v6:
time: 133 us; the launch traced here: 132 us
  Pallas kernels  131 us (98%)
    pallas_call x1, Pallas kernels, device_block(): pl.pallas_call(functools.partial(kernel, n_cols), out_shape=pltpu.VMEM((r...  131 us

profile of v6, /device:TPU:0, one launch (start us, length us, event | category | flops | bytes accessed | tf_op | source)
XLA Modules:
  0.0 132.3 jit_solution(14014501250918183747)
XLA Ops:
  0.0 131.3 %product.1 = bf16[128,4608]{1,0:T(8,128)(2,1)S(1)} custom-call(bf16[128,8192]{1,0:T(8,128)(2,1)} %a_ref.1, bf16[256,4608]{1,0:T(8,128)(2,1)} %b_ref.1), custom_call_target="tpu_custom_call" | custom-call | tf_op jit(solution)/shard_map/product/pallas_call | solution.py:471
  131.3 1.0 copy.4

commit v7 on v6

--- a/solution.py
+++ b/solution.py
@@ -11,19 +11,20 @@
 MESH = pl.DeviceIdType.MESH
 NC, SMALL = 256, 128
 N_SMALL = 0
+HALF = 2
 SHARED = 5
 JOBS = 4
 FIRST_JOB, JOB_PERIOD = 4, 3
 AHEAD = 2
 AHEAD_END = 5
-A2_FIRST = 3
+A2_FIRST, A2_BURST = 3, 4
 A2_STEPS = {5: 4, 7: 5, 9: 6, 11: 7}
 LAG_MULTIPLY = (1, 1)
 LAG_MIDDLE, LAG_FINISH = (1, 1), (3, 3)
 LAG_JOB_MIDDLE, LAG_JOB_FINISH = 2, 4
-RING_Z, RING = 12, 8
+RING_Z, RING = 8, 6
 EXTRA = (12,)
-BACK = 17
+BACK = 18
 
 Chunk = collections.namedtuple("Chunk", "j start width")
 
@@ -128,12 +129,15 @@
     def await_got(ref, sem):
         remote(ref, ref, loc.at[0], sem, twin).wait_recv()
 
-    def a_copy(i, k):
+    def a_half(h):
+        return pl.ds(h * hr, hr)
+
+    def a_copy(i, k, h):
         px, py = plane_xy[i]
-        return remote(a_ref.at[:, a_cols(px, py, k)], abuf.at[2 * x + y, :, pl.ds(k * half, half)], a_snd.at[0], a_rcv.at[0], plane[i])
-
-    def get_a():
-        await_got(abuf.at[pl.ds(0, 3)], a_rcv.at[0])
+        return remote(a_ref.at[a_half(h), a_cols(px, py, k)], abuf.at[2 * x + y, a_half(h), pl.ds(k * half, half)], a_snd.at[0], a_rcv.at[h], plane[i])
+
+    def get_a(h):
+        await_got(abuf.at[pl.ds(0, 3), a_half(h)], a_rcv.at[h])
 
     def job_rows(i):
         return pl.ds(pl.multiple_of(i * jr, jr), jr)
@@ -245,12 +249,17 @@
         twin_part(c, 1 - core, 0, half).wait_recv()
 
     def view(own, j):
+        if own == HALF:
+            q = hr // 2
+            return pbuf, (rx, ry), (sx, sy), pl.ds(j * hr, q), pl.ds(j * hr + q, q), pl.ds(j * q, q), pl.ds(0, NC)
         if own:
             return pbuf, (rx, ry), (sx, sy), pl.ds(0, hr), pl.ds(hr, hr), pl.ds(0, hr), cols(j)
         lo = pl.multiple_of(j * jr, jr)
         return pbuf2, (rx2, ry2), (sx2, sy2), pl.ds(lo, jr // 2), pl.ds(pl.multiple_of(lo + jr // 2, jr // 2), jr // 2), pl.ds(pl.multiple_of(j * (jr // 2), jr // 2), jr // 2), pl.ds(0, wide)
 
     def sems(own, j):
+        if own == HALF:
+            return r_snd.at[0], r_rcv.at[RING + j], q_snd.at[0], q_rcv.at[RING + j]
         if own:
             return r_snd.at[0], r_rcv.at[j.j % RING], q_snd.at[0], q_rcv.at[j.j % RING]
         return rj_snd.at[0], rj_rcv.at[j], qj_snd.at[0], qj_rcv.at[j]
@@ -276,16 +285,28 @@
         await_got(p.at[0, :, low, cs], sems(own, j)[3])
         top = p[x, y, low, cs] + bx[y, rs, cs] + qy[rs, cs]
         bottom = p[x, y, high, cs] + by[x, rs, cs] + qx[rs, cs]
-        rows = pl.ds(0, rows_a) if own else job_rows(j)
+        rows = a_half(j) if own == HALF else pl.ds(0, rows_a) if own else job_rows(j)
         out[rows, cs] = jnp.concatenate([top, bottom], axis=0).astype(out.dtype)
 
     def c_copy(i):
         return remote(cbuf.at[job_rows(i)], c_ref.at[job_rows(i), pl.ds(0, wide)], c_snd.at[0], c_rcv.at[0], partner)
 
+    def starts(c):
+        return inner & (c.j == 0)
+
     def multiply(c):
-        when(inner, c.j == 0)(get_a)
-
-        @when(works(c))
+        @when(starts(c))
+        def _():
+            get_a(0)
+            get_twin(c)
+            for h in range(2):
+                if h == 1:
+                    get_a(1)
+                a = abuf[:, a_half(h), :].reshape(4 * hr, 2 * half)
+                pbuf[:, :, a_half(h), pl.ds(0, NC)] = jnp.dot(a, bbuf[:, pl.ds(0, NC)], preferred_element_type=f32).reshape(2, 2, hr, NC)
+                first_stage(HALF, h)
+
+        @when(works(c), ~starts(c))
         def _():
             get_twin(c)
             a = abuf[...].reshape(4 * rows_a, 2 * half)
@@ -293,12 +314,20 @@
             first_stage(True, c)
 
     def own_middle(c):
-        when(works(c))(lambda: middle(True, c))
+        @when(starts(c))
+        def _():
+            middle(HALF, 0)
+            middle(HALF, 1)
+
+        when(works(c), ~starts(c))(lambda: middle(True, c))
 
     def own_finish(c):
-        @when(works(c))
-        def _():
-            finish(True, c)
+        @when(starts(c))
+        def _():
+            finish(HALF, 0)
+            finish(HALF, 1)
+
+        when(works(c), ~starts(c))(lambda: finish(True, c))
 
     def job_multiply(i):
         await_got(abuf2.at[:, job_rows(i)], a2_rcv.at[i])
@@ -329,9 +358,10 @@
         m = m - FIRST_JOB
         when(inner, m >= 0, m % JOB_PERIOD == 0, m < JOBS * JOB_PERIOD)(lambda: fn(m // JOB_PERIOD))
 
-    for i in range(3):
-        for k in range(2):
-            a_copy(i, k).start()
+    for h in range(2):
+        for i in range(3):
+            for k in range(2):
+                a_copy(i, k, h).start()
     load_b.wait()
 
     @when(inner)
@@ -384,8 +414,9 @@
 
         @when(end, t == A2_FIRST)
         def _():
-            get_a()
-            for i in range(4):
+            get_a(0)
+            get_a(1)
+            for i in range(A2_BURST):
                 a2_copy(i).start()
 
         first_hops(r)
@@ -484,9 +515,9 @@
                 pltpu.VMEM((2, hr, nj), f32), pltpu.VMEM((2, hr, nj), f32),
                 pltpu.VMEM((hr, nj), f32), pltpu.VMEM((hr, nj), f32),
                 pltpu.VMEM((rows, nj), bf16),
-                dma((3,)), dma((1,)), dma((JOBS,)),
+                dma((3,)), dma((2,)), dma((JOBS,)),
                 dma((n,)), dma((RING_Z,)), dma((1,)), dma((2, RING_Z)),
-                dma((RING,)), dma((RING,)), dma((RING,)), dma((JOBS,)), dma((JOBS,)), dma((1,)),
+                dma((RING,)), dma((RING + 2,)), dma((RING + 2,)), dma((JOBS,)), dma((JOBS,)), dma((1,)),
                 dma((1,)), dma((1,)), dma((3,)), dma((3,)),
                 dma((1,)), dma((1,)), dma((1,)), dma((1,)), dma((1,)), dma((1,)),
             ],

time: 133 us -> 132 us (level)
  no operation moved by 1% of the time
where the time goes in v7:
time: 132 us
  Pallas kernels  131 us (99%)
    pallas_call x1, Pallas kernels, device_block(): pl.pallas_call(functools.partial(kernel, n_cols), out_shape=pltpu.VMEM((r...  131 us

profile of v7, /device:TPU:0, one launch (start us, length us, event | category | flops | bytes accessed | tf_op | source)
XLA Modules:
  0.0 131.7 jit_solution(3868826452273298546)
XLA Ops:
  0.0 130.7 %product.1 = bf16[128,4608]{1,0:T(8,128)(2,1)S(1)} custom-call(bf16[128,8192]{1,0:T(8,128)(2,1)} %a_ref.1, bf16[256,4608]{1,0:T(8,128)(2,1)} %b_ref.1), custom_call_target="tpu_custom_call" | custom-call | tf_op jit(solution)/shard_map/product/pallas_call | solution.py:502
  130.7 1.0 copy.4

commit v8 on v7

--- a/solution.py
+++ b/solution.py
@@ -23,7 +23,7 @@
 LAG_MIDDLE, LAG_FINISH = (1, 1), (3, 3)
 LAG_JOB_MIDDLE, LAG_JOB_FINISH = 2, 4
 RING_Z, RING = 8, 6
-EXTRA = (12,)
+EXTRA = (12, 16)
 BACK = 18
 
 Chunk = collections.namedtuple("Chunk", "j start width")
@@ -358,10 +358,9 @@
         m = m - FIRST_JOB
         when(inner, m >= 0, m % JOB_PERIOD == 0, m < JOBS * JOB_PERIOD)(lambda: fn(m // JOB_PERIOD))
 
-    for h in range(2):
-        for i in range(3):
-            for k in range(2):
-                a_copy(i, k, h).start()
+    for i in range(3):
+        for k in range(2):
+            a_copy(i, k, 0).start()
     load_b.wait()
 
     @when(inner)
@@ -383,6 +382,9 @@
     def _():
         outward(z, dn_snd.at[0], down).start()
 
+    for i in range(3):
+        for k in range(2):
+            a_copy(i, k, 1).start()
     for k in range(2):
         load_a[k].wait()
 

time: 132 us -> 131 us (level)
  no operation moved by 1% of the time
where the time goes in v8:
time: 131 us
  Pallas kernels  130 us (99%)
    pallas_call x1, Pallas kernels, device_block(): pl.pallas_call(functools.partial(kernel, n_cols), out_shape=pltpu.VMEM((r...  130 us

profile of v8, /device:TPU:0, one launch (start us, length us, event | category | flops | bytes accessed | tf_op | source)
XLA Modules:
  0.0 131.3 jit_solution(14070335495420211520)
XLA Ops:
  0.0 130.3 %product.1 = bf16[128,4608]{1,0:T(8,128)(2,1)S(1)} custom-call(bf16[128,8192]{1,0:T(8,128)(2,1)} %a_ref.1, bf16[256,4608]{1,0:T(8,128)(2,1)} %b_ref.1), custom_call_target="tpu_custom_call" | custom-call | tf_op jit(solution)/shard_map/product/pallas_call | solution.py:504
  130.3 1.0 copy.4

commit v9 on v8

--- a/solution.py
+++ b/solution.py
@@ -275,8 +275,8 @@
         _, got, snd, rcv = sems(own, j)
         await_got(p.at[:, :, low, cs], got)
         p[x, 1 - y, low, cs] += bx[1 - y, rs, cs]
+        remote(p.at[x, 1 - y, low, cs], qy.at[rs, cs], snd, rcv, y_peer).start()
         p[1 - x, y, high, cs] += by[1 - x, rs, cs]
-        remote(p.at[x, 1 - y, low, cs], qy.at[rs, cs], snd, rcv, y_peer).start()
         remote(p.at[1 - x, y, high, cs], qx.at[rs, cs], snd, rcv, x_peer).start()
 
     def finish(own, j):

time: 131 us -> 131 us (level)
  no operation moved by 1% of the time
where the time goes in v9:
time: 131 us
  Pallas kernels  130 us (99%)
    pallas_call x1, Pallas kernels, device_block(): pl.pallas_call(functools.partial(kernel, n_cols), out_shape=pltpu.VMEM((r...  130 us

profile of v9, /device:TPU:0, one launch (start us, length us, event | category | flops | bytes accessed | tf_op | source)
XLA Modules:
  0.0 131.3 jit_solution(2313336809941650564)
XLA Ops:
  0.0 130.3 %product.1 = bf16[128,4608]{1,0:T(8,128)(2,1)S(1)} custom-call(bf16[128,8192]{1,0:T(8,128)(2,1)} %a_ref.1, bf16[256,4608]{1,0:T(8,128)(2,1)} %b_ref.1), custom_call_target="tpu_custom_call" | custom-call | tf_op jit(solution)/shard_map/product/pallas_call | solution.py:504
  130.3 1.0 copy.4
